TPU v7x, 32 devices: a whole 2x2x4 slice. The times are simulated.
32 devices in a mesh: ba: 8 (over z, core), ha: 4 (over y, x).
Axes of the slice: x: 2, y: 2, z: 4, core: 2. Of those that a mesh axis runs over, the one named last changes fastest.
Arguments:
- queries: bfloat16 [2048, 64, 576], P('ba', 'ha'), may hold values from -6 to 6
- out_grad: bfloat16 [2048, 64, 512], P('ba', 'ha'), may hold values from -1.1953125 to 1.1953125
- out_saved: bfloat16 [2048, 64, 512], P('ba', 'ha'), may hold values from -3 to 3
- logsumexp: float32 [2048, 64], P('ba', 'ha'), may hold values from 7 to 9
- parents: int32 [2048], P('ba'), may hold values from 0 to 511, as said below
- latents: bfloat16 [512, 576], P(('ba', 'ha')), may hold values from -6 to 6
- hidden: bfloat16 [512, 7168], P('ba', 'ha'), may hold values from -6 to 6
- latent_weight: bfloat16 [576, 7168], P(None, 'ha'), may hold values from -0.0625 to 0.0625
Outputs:
- query_grad: bfloat16 [2048, 64, 576], P('ba', 'ha')
- weight_grad: bfloat16 [576, 7168], P('ba', 'ha')
- input_grad: bfloat16 [512, 7168], P('ba', 'ha')
Inputs may be any that keep to these rules, and one draw needn't show every extreme that they name: `parents`: the 32 tokens of each aligned block of 32 share one value; some token has 0 and some has 511.
All inputs are finite; a program needn't handle non-finite values.
Results may differ from a plain program's by a relative error of at most 0.0067.
Values may be sent and summed in bfloat16 or wider, within the bound.
No kernel may reach another device: no remote copies, remote signals or barrier semaphores. Data moves between devices by JAX's collectives and lax.ppermute only.
A program may use at most 64 MiB of HBM per device.

v0:
```python
import jax
import jax.numpy as jnp
from jax import lax
from jax.sharding import PartitionSpec as P

RANK = 512
ROPE = 64
softmax_scale = 192.0 ** (-0.5)


def tile_terms(query_rows, grad_rows, lse_rows, deltas, limits, key_block, offset):
    key_count = key_block.shape[0]
    key_index = offset + jnp.arange(key_count, dtype=jnp.int32)
    scores = (
        jnp.einsum("qd,kd->qk", query_rows, key_block, preferred_element_type=jnp.float32)
        * softmax_scale
    )
    visible = key_index[None, :] <= limits[:, None]
    weights = jnp.where(visible, jnp.exp(scores - lse_rows[:, None]), jnp.float32(0.0))
    grad_prob = jnp.einsum(
        "qd,kd->qk", grad_rows, key_block[:, :RANK], preferred_element_type=jnp.float32
    )
    grad_score = (weights * (grad_prob - deltas[:, None])).astype(jnp.bfloat16)
    query_part = jnp.einsum("qk,kd->qd", grad_score, key_block, preferred_element_type=jnp.float32)
    value_part = jnp.einsum(
        "qk,qd->kd", weights.astype(jnp.bfloat16), grad_rows, preferred_element_type=jnp.float32
    )
    key_grad = softmax_scale * jnp.einsum(
        "qk,qd->kd", grad_score, query_rows, preferred_element_type=jnp.float32
    )
    key_grad = key_grad + jnp.pad(value_part, ((0, 0), (0, ROPE)))
    return (query_part, key_grad)


def on_device(queries, out_grad, out_saved, logsumexp, parents, latents, hidden, latent_weight):
    tokens_here, heads_here, full_width = queries.shape
    row_total = tokens_here * heads_here
    query_rows = queries.reshape(row_total, full_width)
    grad_rows = out_grad.reshape(row_total, RANK)
    saved_rows = out_saved.reshape(row_total, RANK)
    lse_rows = logsumexp.reshape(row_total)
    limits = jnp.repeat(parents, heads_here)
    deltas = jnp.sum(saved_rows.astype(jnp.float32) * grad_rows.astype(jnp.float32), axis=1)
    all_keys = lax.all_gather(latents, ("ba", "ha"), axis=0, tiled=True)
    prefix_total = all_keys.shape[0]
    tile_len = min(256, prefix_total)
    tile_count = prefix_total // tile_len
    key_tiles = all_keys.reshape(tile_count, tile_len, full_width)
    offsets = jnp.arange(tile_count, dtype=jnp.int32) * tile_len

    def tile_step(query_acc, tile_inputs):
        key_block, offset = tile_inputs
        query_part, key_grad = tile_terms(
            query_rows, grad_rows, lse_rows, deltas, limits, key_block, offset
        )
        return (query_acc + query_part, key_grad)

    query_acc, key_stack = lax.scan(
        tile_step, jnp.zeros((row_total, full_width), jnp.float32), (key_tiles, offsets)
    )
    latent_acc = key_stack.reshape(prefix_total, full_width)
    query_grad = (
        (softmax_scale * query_acc)
        .astype(jnp.bfloat16)
        .reshape(tokens_here, heads_here, full_width)
    )
    branch_part = lax.psum_scatter(latent_acc, "ba", scatter_dimension=0, tiled=True)
    row_grads = lax.psum(branch_part, "ha").astype(jnp.bfloat16)
    weight_grad = lax.psum_scatter(
        jnp.einsum("pl,ph->lh", row_grads, hidden, preferred_element_type=jnp.float32),
        "ba",
        scatter_dimension=0,
        tiled=True,
    ).astype(jnp.bfloat16)
    input_grad = jnp.dot(row_grads, latent_weight, preferred_element_type=jnp.float32).astype(
        jnp.bfloat16
    )
    return (query_grad, weight_grad, input_grad)


def solution(mesh):
    return jax.shard_map(
        on_device,
        mesh=mesh,
        in_specs=(
            P("ba", "ha", None),
            P("ba", "ha", None),
            P("ba", "ha", None),
            P("ba", "ha"),
            P("ba"),
            P(("ba", "ha"), None),
            P("ba", "ha"),
            P(None, "ha"),
        ),
        out_specs=(P("ba", "ha", None), P("ba", "ha"), P("ba", "ha")),
        check_vma=False,
    )
```

profile of v0, /device:TPU:0, one launch (start us, length us, event | category | flops | bytes accessed | tf_op | source)
XLA Modules:
  0.0 245.1 jit_solution(18365195262082448630)
XLA Ops:
  7.3 0.9 copy.21
  8.3 4.6 %multiply_reduce_fusion = f32[256,16]{1,0:T(8,128)S(1)} fusion(bf16[256,16,512]{2,1,0:T(8,128)(2,1)} %param.11, bf16[256,16,512]{2,1,0:T(8,128)(2,1)} %param.12), kind=kLoop, calls=%fused_computation.21 | loop fusion | flops 8384512 | bytes 8404992 | tf_op jit(solution)/shard_map/reduce_sum | solution.py:43
  13.1 73.2 %all_gather.3 = bf16[512,576]{1,0:T(8,128)(2,1)S(1)} all-gather(bf16[16,576]{1,0:T(8,128)(2,1)S(1)} %copy-done.8), channel_id=1, replica_groups=mesh['ba'=8,'ha'=4] {'ba','ha'}, dimensions={0}, use_global_device_ids=true | all-gather | bytes 608256 | tf_op jit(solution)/shard_map/all_gather | solution.py:44
  86.3 9.0 %copy.20 = bf16[256,16,576]{2,1,0:T(8,128)(2,1)} copy(bf16[256,16,576]{0,2,1:T(8,128)(2,1)} %param.10) | data formatting | bytes 9437184 | tf_op args[0]
  95.2 36.9 %while.16 = (s32[]{:T(128)}, f32[4096,576]{0,1:T(8,128)}, f32[2,256,576]{1,2,0:T(8,128)}, s32[2]{0:T(128)S(1)}, bf16[2,256,576]{2,1,0:T(8,128)(2,1)S(1)}, /*inde...) while((s32[]{:T(128)}, f32[4096,576]{0,1:T(8,128)}, ...), condition=%wide.wide.region_2.3_spmd.clone, body=%wide.wide.region_1.2_spmd.clone.sunk | while | flops 5784764416 | bytes 167284112 | solution.py:58
  95.2 0.6 dynamic_slice.22
  95.8 0.6 iota_add_fusion.3
  96.7 4.6 %fusion.69 = f32[4096,256]{0,1:T(8,128)S(1)} fusion(bf16[256,576]{1,0:T(8,128)(2,1)S(1)} %dynamic-slice_bitcast_fusion.3, bf16[4096,576]{1,0:T(8,128)(2,1)} %get-tuple-element.351, f32[4096]{0:T(1024)S(1)} %get-tuple-element.356, s32[4096]{0:T(1024)S(1)} %le.46, s32[256]{0:T(256)S(1)} %iota_add_fusion.3), kind=kOutput, calls=%fused_computation.9.clone.clone.1 | convolution fusion | flops 1212153856 | bytes 9241600 | tf_op jit(solution)/shard_map/while/body/eval_jaxpr/qd,kd->qk/dot_general | solution.py:15
  101.4 1.8 fusion.71
  103.2 1.3 fusion.70
  104.6 2.1 fusion.72
  107.5 2.6 %select_add_fusion.3 = f32[4096,576]{0,1:T(8,128)S(1)} fusion(f32[4096,576]{0,1:T(8,128)S(1)} %bitcast.75, bf16[4096,256]{0,1:T(8,128)(2,1)S(1)} %fusion.70, bf16[256,576]{1,0:T(8,128)(2,1)S(1)} %dynamic-slice_bitcast_fusion.3, pred[]{:T(512)S(6)} %compare.5), kind=kOutput, calls=%fused_computation.1.clone.clone.1 | convolution fusion | flops 1212678144 | bytes 21266432 | tf_op jit(solution)/shard_map/while/body/eval_jaxpr/qk,kd->qd/dot_general | solution.py:24
  110.0 3.7 %copy-done.1 = f32[4096,576]{0,1:T(8,128)} copy-done((f32[4096,576]{0,1:T(8,128)}, f32[4096,576]{0,1:T(8,128)S(1)}, u32[]{:S(2)}) %copy-start.1) | copy-done | bytes 9437208 | tf_op jit(solution)/shard_map/while
  113.7 0.6 dynamic_slice.22
  114.3 0.6 iota_add_fusion.3
  115.2 4.6 %fusion.69 = f32[4096,256]{0,1:T(8,128)S(1)} fusion(bf16[256,576]{1,0:T(8,128)(2,1)S(1)} %dynamic-slice_bitcast_fusion.3, bf16[4096,576]{1,0:T(8,128)(2,1)} %get-tuple-element.351, f32[4096]{0:T(1024)S(1)} %get-tuple-element.356, s32[4096]{0:T(1024)S(1)} %le.46, s32[256]{0:T(256)S(1)} %iota_add_fusion.3), kind=kOutput, calls=%fused_computation.9.clone.clone.1 | convolution fusion | flops 1212153856 | bytes 9241600 | tf_op jit(solution)/shard_map/while/body/eval_jaxpr/qd,kd->qk/dot_general | solution.py:15
  119.8 1.8 fusion.71
  121.7 1.3 fusion.70
  123.0 2.1 fusion.72
  125.9 2.6 %select_add_fusion.3 = f32[4096,576]{0,1:T(8,128)S(1)} fusion(f32[4096,576]{0,1:T(8,128)S(1)} %bitcast.75, bf16[4096,256]{0,1:T(8,128)(2,1)S(1)} %fusion.70, bf16[256,576]{1,0:T(8,128)(2,1)S(1)} %dynamic-slice_bitcast_fusion.3, pred[]{:T(512)S(6)} %compare.5), kind=kOutput, calls=%fused_computation.1.clone.clone.1 | convolution fusion | flops 1212678144 | bytes 21266432 | tf_op jit(solution)/shard_map/while/body/eval_jaxpr/qk,kd->qd/dot_general | solution.py:24
  128.5 3.7 %copy-done.1 = f32[4096,576]{0,1:T(8,128)} copy-done((f32[4096,576]{0,1:T(8,128)}, f32[4096,576]{0,1:T(8,128)S(1)}, u32[]{:S(2)}) %copy-start.1) | copy-done | bytes 9437208 | tf_op jit(solution)/shard_map/while
  132.2 2.8 %copy.28 = f32[2,256,576]{2,1,0:T(8,128)} copy(f32[2,256,576]{1,2,0:T(8,128)} %get-tuple-element.130) | data formatting | bytes 2359296
  135.2 29.1 %reduce-scatter.7.cloned.1.call-done = f32[64,576]{1,0:T(8,128)} async-done(((f32[512,576]{1,0:T(8,128)}), f32[64,576]{1,0:T(8,128)}) %reduce-scatter.7.cloned.1.call-update) | async-done | bytes 147472
  164.3 1.1 copy.27
  165.3 20.5 %all-reduce.2 = bf16[64,576]{0,1:T(8,128)(2,1)S(1)} all-reduce(f32[64,576]{0,1:T(8,128)S(1)} %copy.27), channel_id=1, replica_groups=mesh['ba'=8,'ha'=4] {'ha'}, use_global_device_ids=true, to_apply=%region_4.5 | all-reduce | flops 36864 | bytes 221184 | tf_op jit(solution)/shard_map/psum | solution.py:68
  185.9 2.7 %fusion.18 = f32[576,1792]{1,0:T(8,128)} fusion(bf16[64,576]{0,1:T(8,128)(2,1)S(1)} %all-reduce.2, bf16[64,1792]{1,0:T(8,128)(2,1)S(1)} %copy-done.6), kind=kOutput, calls=%fused_computation.27 | convolution fusion | flops 132120576 | bytes 4431872 | tf_op jit(solution)/shard_map/pl,ph->lh/dot_general | solution.py:70
  188.6 7.0 %multiply_convert_fusion = bf16[4096,576]{0,1:T(8,128)(2,1)} fusion(f32[4096,576]{0,1:T(8,128)} %get-tuple-element.129), kind=kLoop, calls=%fused_computation.20 | loop fusion | flops 4718592 | bytes 14155776 | tf_op jit(solution)/shard_map/convert_element_type | solution.py:64
  195.7 7.6 %copy.22 = bf16[4096,576]{1,0:T(8,128)(2,1)} copy(bf16[4096,576]{0,1:T(8,128)(2,1)} %multiply_convert_fusion) | data formatting | bytes 9437184 | tf_op jit(solution)/shard_map/convert_element_type | solution.py:64
  203.3 8.2 %copy.24 = bf16[256,16,576]{0,2,1:T(8,128)(2,1)} copy(bf16[256,16,576]{2,1,0:T(8,128)(2,1)} %bitcast.77) | data formatting | bytes 9437184
  211.5 1.2 convolution_convert_fusion
  212.8 23.7 %reduce-scatter.5.cloned.1.call-done = f32[72,1792]{1,0:T(8,128)} async-done(((f32[576,1792]{1,0:T(8,128)}), f32[72,1792]{1,0:T(8,128)}) %reduce-scatter.5.cloned.1.call-update) | async-done | bytes 516112 | tf_op jit(solution)/shard_map/reduce_scatter | solution.py:69
  236.5 1.8 convert_element_type.40
  (63 shorter events, 2.5 us)
Async XLA Ops:
  7.2 204.4 %copy-start = (bf16[576,1792]{1,0:T(8,128)(2,1)S(1)}, bf16[576,1792]{1,0:T(8,128)(2,1)}, u32[]{:S(2)}) copy-start(bf16[576,1792]{1,0:T(8,128)(2,1)} %param.17) | copy-start | bytes 6193156
  7.2 157.1 %reduce-scatter.7.cloned.1.call-start = ((), (), s32[]{:S(2)}) async-start(), calls=%async_computation.3 | async-start | bytes 1474560
  8.2 4.8 %copy-start.5 = (f32[256,16]{1,0:T(8,128)}, f32[256,16]{1,0:T(8,128)S(1)}, u32[]{:S(2)}) copy-start(f32[256,16]{1,0:T(8,128)S(1)} %copy.21) | copy-start | bytes 49156
  8.3 4.8 %copy-start.8 = (bf16[16,576]{1,0:T(8,128)(2,1)S(1)}, bf16[16,576]{1,0:T(8,128)(2,1)}, u32[]{:S(2)}) copy-start(bf16[16,576]{1,0:T(8,128)(2,1)} %param.15) | copy-start | bytes 55300
  86.3 9.0 %copy-start.7 = (s32[256]{0:T(256)S(1)}, s32[256]{0:T(256)}, u32[]{:S(2)}) copy-start(s32[256]{0:T(256)} %param.14) | copy-start | bytes 3076
  96.7 4.6 %copy-start.2 = (bf16[4096,512]{1,0:T(8,128)(2,1)S(1)}, bf16[4096,512]{1,0:T(8,128)(2,1)}, u32[]{:S(2)}) copy-start(bf16[4096,512]{1,0:T(8,128)(2,1)} %get-tuple-element.353) | copy-start | bytes 12582916 | tf_op jit(solution)/shard_map/while
  96.7 7.8 %slice-start.3 = ((s8[5242880]{0:T(1024)(128)(4,1)}), s8[4194304]{0:T(1024)(128)(4,1)S(1)}, s32[]{:S(2)}) async-start(s8[5242880]{0:T(1024)(128)(4,1)} %bitcast.80), calls=%async_computation.7 | async-start | bytes 8388608 | tf_op jit(solution)/shard_map/while
  101.4 3.2 %slice-start.4 = ((s8[5242880]{0:T(1024)(128)(4,1)}), s8[1048576]{0:T(1024)(128)(4,1)S(1)}, s32[]{:S(2)}) async-start(s8[5242880]{0:T(1024)(128)(4,1)} %bitcast.80), calls=%async_computation.8 | async-start | bytes 2097152 | tf_op jit(solution)/shard_map/while
  103.2 1.4 copy-start.3
  103.2 3.5 %slice-start = ((s8[9437184]{0:T(1024)(128)(4,1)}), s8[4194304]{0:T(1024)(128)(4,1)S(1)}, s32[]{:S(2)}) async-start(s8[9437184]{0:T(1024)(128)(4,1)} %bitcast.74), calls=%async_computation.4 | async-start | bytes 8388608 | tf_op jit(solution)/shard_map/while
  103.2 3.8 %slice-start.1 = ((s8[9437184]{0:T(1024)(128)(4,1)}), s8[4194304]{0:T(1024)(128)(4,1)S(1)}, s32[]{:S(2)}) async-start(s8[9437184]{0:T(1024)(128)(4,1)} %bitcast.74), calls=%async_computation.5 | async-start | bytes 8388608 | tf_op jit(solution)/shard_map/while
  104.6 2.9 %slice-start.2 = ((s8[9437184]{0:T(1024)(128)(4,1)}), s8[1048576]{0:T(1024)(128)(4,1)S(1)}, s32[]{:S(2)}) async-start(s8[9437184]{0:T(1024)(128)(4,1)} %bitcast.74), calls=%async_computation.6 | async-start | bytes 2097152 | tf_op jit(solution)/shard_map/while
  107.5 2.6 %copy-start.4 = (f32[2,256,576]{1,2,0:T(8,128)}, f32[2,256,576]{1,2,0:T(8,128)S(1)}, u32[]{:S(2)}) copy-start(f32[2,256,576]{1,2,0:T(8,128)S(1)} %fusion.72) | copy-start | bytes 3538948 | tf_op jit(solution)/shard_map/while
  110.0 3.7 %copy-start.1 = (f32[4096,576]{0,1:T(8,128)}, f32[4096,576]{0,1:T(8,128)S(1)}, u32[]{:S(2)}) copy-start(f32[4096,576]{0,1:T(8,128)S(1)} %select_add_fusion.3) | copy-start | bytes 28311556 | tf_op jit(solution)/shard_map/while
  115.2 4.6 %copy-start.2 = (bf16[4096,512]{1,0:T(8,128)(2,1)S(1)}, bf16[4096,512]{1,0:T(8,128)(2,1)}, u32[]{:S(2)}) copy-start(bf16[4096,512]{1,0:T(8,128)(2,1)} %get-tuple-element.353) | copy-start | bytes 12582916 | tf_op jit(solution)/shard_map/while
  115.2 7.8 %slice-start.3 = ((s8[5242880]{0:T(1024)(128)(4,1)}), s8[4194304]{0:T(1024)(128)(4,1)S(1)}, s32[]{:S(2)}) async-start(s8[5242880]{0:T(1024)(128)(4,1)} %bitcast.80), calls=%async_computation.7 | async-start | bytes 8388608 | tf_op jit(solution)/shard_map/while
  119.8 3.2 %slice-start.4 = ((s8[5242880]{0:T(1024)(128)(4,1)}), s8[1048576]{0:T(1024)(128)(4,1)S(1)}, s32[]{:S(2)}) async-start(s8[5242880]{0:T(1024)(128)(4,1)} %bitcast.80), calls=%async_computation.8 | async-start | bytes 2097152 | tf_op jit(solution)/shard_map/while
  121.7 1.4 copy-start.3
  121.7 3.5 %slice-start = ((s8[9437184]{0:T(1024)(128)(4,1)}), s8[4194304]{0:T(1024)(128)(4,1)S(1)}, s32[]{:S(2)}) async-start(s8[9437184]{0:T(1024)(128)(4,1)} %bitcast.74), calls=%async_computation.4 | async-start | bytes 8388608 | tf_op jit(solution)/shard_map/while
  121.7 3.8 %slice-start.1 = ((s8[9437184]{0:T(1024)(128)(4,1)}), s8[4194304]{0:T(1024)(128)(4,1)S(1)}, s32[]{:S(2)}) async-start(s8[9437184]{0:T(1024)(128)(4,1)} %bitcast.74), calls=%async_computation.5 | async-start | bytes 8388608 | tf_op jit(solution)/shard_map/while
  123.0 2.9 %slice-start.2 = ((s8[9437184]{0:T(1024)(128)(4,1)}), s8[1048576]{0:T(1024)(128)(4,1)S(1)}, s32[]{:S(2)}) async-start(s8[9437184]{0:T(1024)(128)(4,1)} %bitcast.74), calls=%async_computation.6 | async-start | bytes 2097152 | tf_op jit(solution)/shard_map/while
  125.9 2.6 %copy-start.4 = (f32[2,256,576]{1,2,0:T(8,128)}, f32[2,256,576]{1,2,0:T(8,128)S(1)}, u32[]{:S(2)}) copy-start(f32[2,256,576]{1,2,0:T(8,128)S(1)} %fusion.72) | copy-start | bytes 3538948 | tf_op jit(solution)/shard_map/while
  128.5 3.7 %copy-start.1 = (f32[4096,576]{0,1:T(8,128)}, f32[4096,576]{0,1:T(8,128)S(1)}, u32[]{:S(2)}) copy-start(f32[4096,576]{0,1:T(8,128)S(1)} %select_add_fusion.3) | copy-start | bytes 28311556 | tf_op jit(solution)/shard_map/while
  132.2 53.7 %copy-start.6 = (bf16[64,1792]{1,0:T(8,128)(2,1)S(1)}, bf16[64,1792]{1,0:T(8,128)(2,1)}, u32[]{:S(2)}) copy-start(bf16[64,1792]{1,0:T(8,128)(2,1)} %param.16) | copy-start | bytes 688132
  135.0 101.5 %reduce-scatter.5.cloned.1.call-start = ((), (), s32[]{:S(2)}) async-start(), calls=%async_computation.2 | async-start | bytes 4644864 | tf_op jit(solution)/shard_map/reduce_scatter | solution.py:69
Sparse Core Ops, SparseCore 0:
  135.1 29.1 reduce-scatter.6
  188.8 47.6 reduce-scatter.4
where the time goes:
time: 246 us; the launch traced here: 245 us
  blocking collectives  93.7 us (38%)
  waiting for transfers between devices  52.8 us (21%)
  local copies, waits for them, and re-layouts  40.3 us (16%)
  matrix products  28.7 us (12%)
  other arithmetic  14.7 us (6%)
  between operations  14.1 us (6%)
    all_gather x1, blocking collectives, on_device(): all_keys = lax.all_gather(latents, ('ba', 'ha'), axis=0, tiled=True)  73.2 us
    unnamed x3, waiting for transfers between devices  29.1 us
    reduce_scatter x1, waiting for transfers between devices, on_device(): lax.psum_scatter(jnp.einsum('pl,ph->lh', row_grads, hidden, preferred_ele...  23.7 us
    unnamed x15, local copies, waits for them, and re-layouts  22 us
    psum x1, blocking collectives, on_device(): row_grads = lax.psum(branch_part, 'ha').astype(jnp.bfloat16)  20.5 us
    dot_general x2, matrix products, tile_terms(): jnp.einsum('qd,kd->qk', query_rows, key_block, preferred_element_type=jnp...  9.21 us
    while x36, local copies, waits for them, and re-layouts  8.86 us
    convert_element_type x1, local copies, waits for them, and re-layouts, on_device(): query_grad = (softmax_scale * query_acc).astype(jnp.bfloat16).reshape(tok...  7.65 us
  transfers between devices with their start and end apart: 2, of which 2 were waited for; matrix products, arithmetic and copies ran while one was open for 10% of the time, Pallas kernels for 0%

commit v1 on v0

--- a/solution.py
+++ b/solution.py
@@ -65,7 +65,7 @@
         .reshape(tokens_here, heads_here, full_width)
     )
     branch_part = lax.psum_scatter(latent_acc, "ba", scatter_dimension=0, tiled=True)
-    row_grads = lax.psum(branch_part, "ha").astype(jnp.bfloat16)
+    row_grads = jnp.sum(lax.all_gather(branch_part, "ha"), axis=0).astype(jnp.bfloat16)
     weight_grad = lax.psum_scatter(
         jnp.einsum("pl,ph->lh", row_grads, hidden, preferred_element_type=jnp.float32),
         "ba",

time: 246 us -> 235 us (0.955)
  blocking collectives: 93.7 us -> 84.2 us
    unnamed x3 -> x2, waiting for transfers between devices: 29.1 us -> 0.03 us
    reduce_scatter x0 -> x1, waiting for transfers between devices: none -> 29.1 us  [on_device(): lax.psum_scatter(latent_acc, 'ba', scatter_dimension=0, tiled=True)]
    psum x1 -> x0, blocking collectives: 20.5 us -> none  [on_device(): row_grads = lax.psum(branch_part, 'ha').astype(jnp.bfloat16)]
    all_gather x0 -> x1, blocking collectives: none -> 11 us  [on_device(): lax.all_gather(branch_part, 'ha')]
    unnamed x15 -> x14, local copies, waits for them, and re-layouts: 22 us -> 20.9 us
where the time goes in v1:
time: 235 us; the launch traced here: 234 us
  blocking collectives  84.2 us (36%)
  waiting for transfers between devices  52.5 us (22%)
  local copies, waits for them, and re-layouts  39.2 us (17%)
  matrix products  28.7 us (12%)
  other arithmetic  14.8 us (6%)
  between operations  14.1 us (6%)
    all_gather x1, blocking collectives, on_device(): all_keys = lax.all_gather(latents, ('ba', 'ha'), axis=0, tiled=True)  73.2 us
    reduce_scatter x1, waiting for transfers between devices, on_device(): lax.psum_scatter(latent_acc, 'ba', scatter_dimension=0, tiled=True)  29.1 us
    reduce_scatter x1, waiting for transfers between devices, on_device(): lax.psum_scatter(jnp.einsum('pl,ph->lh', row_grads, hidden, preferred_ele...  23.3 us
    unnamed x14, local copies, waits for them, and re-layouts  20.9 us
    all_gather x1, blocking collectives, on_device(): lax.all_gather(branch_part, 'ha')  11 us
    dot_general x2, matrix products, tile_terms(): jnp.einsum('qd,kd->qk', query_rows, key_block, preferred_element_type=jnp...  9.21 us
    while x36, local copies, waits for them, and re-layouts  8.86 us
    convert_element_type x1, local copies, waits for them, and re-layouts, on_device(): query_grad = (softmax_scale * query_acc).astype(jnp.bfloat16).reshape(tok...  7.64 us
  transfers between devices with their start and end apart: 2, of which 2 were waited for; matrix products, arithmetic and copies ran while one was open for 10% of the time, Pallas kernels for 0%

profile of v1, /device:TPU:0, one launch (start us, length us, event | category | flops | bytes accessed | tf_op | source)
XLA Modules:
  0.0 234.2 jit_solution(1713448976704436003)
XLA Ops:
  7.3 0.9 copy.28
  8.3 4.6 %multiply_reduce_fusion = f32[256,16]{1,0:T(8,128)S(1)} fusion(bf16[256,16,512]{2,1,0:T(8,128)(2,1)} %param.11, bf16[256,16,512]{2,1,0:T(8,128)(2,1)} %param.12), kind=kLoop, calls=%fused_computation.21 | loop fusion | flops 8384512 | bytes 8404992 | tf_op jit(solution)/shard_map/reduce_sum | solution.py:43
  13.1 73.2 %all_gather.9 = bf16[512,576]{1,0:T(8,128)(2,1)S(1)} all-gather(bf16[16,576]{1,0:T(8,128)(2,1)S(1)} %copy-done.8), channel_id=1, replica_groups=mesh['ba'=8,'ha'=4] {'ba','ha'}, dimensions={0}, use_global_device_ids=true | all-gather | bytes 608256 | tf_op jit(solution)/shard_map/all_gather | solution.py:44
  86.3 9.0 %copy.27 = bf16[256,16,576]{2,1,0:T(8,128)(2,1)} copy(bf16[256,16,576]{0,2,1:T(8,128)(2,1)} %param.10) | data formatting | bytes 9437184 | tf_op args[0]
  95.2 36.9 %while.16 = (s32[]{:T(128)}, f32[4096,576]{0,1:T(8,128)}, f32[2,256,576]{1,2,0:T(8,128)}, s32[2]{0:T(128)S(1)}, bf16[2,256,576]{2,1,0:T(8,128)(2,1)S(1)}, /*inde...) while((s32[]{:T(128)}, f32[4096,576]{0,1:T(8,128)}, ...), condition=%wide.wide.region_2.3_spmd.clone, body=%wide.wide.region_1.2_spmd.clone.sunk | while | flops 5784764416 | bytes 167284112 | solution.py:58
  95.2 0.6 dynamic_slice.22
  95.8 0.6 iota_add_fusion.3
  96.7 4.6 %fusion.69 = f32[4096,256]{0,1:T(8,128)S(1)} fusion(bf16[256,576]{1,0:T(8,128)(2,1)S(1)} %dynamic-slice_bitcast_fusion.3, bf16[4096,576]{1,0:T(8,128)(2,1)} %get-tuple-element.364, f32[4096]{0:T(1024)S(1)} %get-tuple-element.369, s32[4096]{0:T(1024)S(1)} %le.46, s32[256]{0:T(256)S(1)} %iota_add_fusion.3), kind=kOutput, calls=%fused_computation.9.clone.clone.1 | convolution fusion | flops 1212153856 | bytes 9241600 | tf_op jit(solution)/shard_map/while/body/eval_jaxpr/qd,kd->qk/dot_general | solution.py:15
  101.4 1.8 fusion.71
  103.2 1.3 fusion.70
  104.6 2.1 fusion.72
  107.0 0.5 slice-done.2
  107.5 2.6 %select_add_fusion.3 = f32[4096,576]{0,1:T(8,128)S(1)} fusion(f32[4096,576]{0,1:T(8,128)S(1)} %bitcast.76, bf16[4096,256]{0,1:T(8,128)(2,1)S(1)} %fusion.70, bf16[256,576]{1,0:T(8,128)(2,1)S(1)} %dynamic-slice_bitcast_fusion.3, pred[]{:T(512)S(6)} %compare.5), kind=kOutput, calls=%fused_computation.1.clone.clone.1 | convolution fusion | flops 1212678144 | bytes 21266432 | tf_op jit(solution)/shard_map/while/body/eval_jaxpr/qk,kd->qd/dot_general | solution.py:24
  110.0 3.7 %copy-done.1 = f32[4096,576]{0,1:T(8,128)} copy-done((f32[4096,576]{0,1:T(8,128)}, f32[4096,576]{0,1:T(8,128)S(1)}, u32[]{:S(2)}) %copy-start.1) | copy-done | bytes 9437208 | tf_op jit(solution)/shard_map/while
  113.7 0.6 dynamic_slice.22
  114.3 0.6 iota_add_fusion.3
  115.2 4.6 %fusion.69 = f32[4096,256]{0,1:T(8,128)S(1)} fusion(bf16[256,576]{1,0:T(8,128)(2,1)S(1)} %dynamic-slice_bitcast_fusion.3, bf16[4096,576]{1,0:T(8,128)(2,1)} %get-tuple-element.364, f32[4096]{0:T(1024)S(1)} %get-tuple-element.369, s32[4096]{0:T(1024)S(1)} %le.46, s32[256]{0:T(256)S(1)} %iota_add_fusion.3), kind=kOutput, calls=%fused_computation.9.clone.clone.1 | convolution fusion | flops 1212153856 | bytes 9241600 | tf_op jit(solution)/shard_map/while/body/eval_jaxpr/qd,kd->qk/dot_general | solution.py:15
  119.8 1.8 fusion.71
  121.7 1.3 fusion.70
  123.0 2.1 fusion.72
  125.9 2.6 %select_add_fusion.3 = f32[4096,576]{0,1:T(8,128)S(1)} fusion(f32[4096,576]{0,1:T(8,128)S(1)} %bitcast.76, bf16[4096,256]{0,1:T(8,128)(2,1)S(1)} %fusion.70, bf16[256,576]{1,0:T(8,128)(2,1)S(1)} %dynamic-slice_bitcast_fusion.3, pred[]{:T(512)S(6)} %compare.5), kind=kOutput, calls=%fused_computation.1.clone.clone.1 | convolution fusion | flops 1212678144 | bytes 21266432 | tf_op jit(solution)/shard_map/while/body/eval_jaxpr/qk,kd->qd/dot_general | solution.py:24
  128.5 3.7 %copy-done.1 = f32[4096,576]{0,1:T(8,128)} copy-done((f32[4096,576]{0,1:T(8,128)}, f32[4096,576]{0,1:T(8,128)S(1)}, u32[]{:S(2)}) %copy-start.1) | copy-done | bytes 9437208 | tf_op jit(solution)/shard_map/while
  132.2 2.8 %copy.36 = f32[2,256,576]{2,1,0:T(8,128)} copy(f32[2,256,576]{1,2,0:T(8,128)} %get-tuple-element.130) | data formatting | bytes 2359296
  135.2 29.1 %reduce-scatter.7.cloned.1.call-done = f32[64,576]{1,0:T(8,128)} async-done(((f32[512,576]{1,0:T(8,128)}), f32[64,576]{1,0:T(8,128)}) %reduce-scatter.7.cloned.1.call-update) | async-done | bytes 147472 | tf_op jit(solution)/shard_map/reduce_scatter | solution.py:67
  164.3 11.0 %all-gather = f32[256,576]{1,0:T(8,128)S(1)} all-gather(f32[64,576]{1,0:T(8,128)} %reduce-scatter.7.cloned.1.call-done), channel_id=2, replica_groups=mesh['ba'=8,'ha'=4] {'ha'}, dimensions={0}, use_global_device_ids=true | all-gather | bytes 737280 | tf_op jit(solution)/shard_map/all_gather | solution.py:68
  175.4 2.8 %fusion.18 = f32[576,1792]{1,0:T(8,128)} fusion(bf16[64,576]{1,0:T(8,128)(2,1)S(1)} %reduce_sum.22, bf16[64,1792]{1,0:T(8,128)(2,1)S(1)} %copy-done.6), kind=kOutput, calls=%fused_computation.27 | convolution fusion | flops 132120576 | bytes 4431872 | tf_op jit(solution)/shard_map/pl,ph->lh/dot_general | solution.py:70
  178.2 7.0 %multiply_convert_fusion = bf16[4096,576]{0,1:T(8,128)(2,1)} fusion(f32[4096,576]{0,1:T(8,128)} %get-tuple-element.129), kind=kLoop, calls=%fused_computation.20 | loop fusion | flops 4718592 | bytes 14155776 | tf_op jit(solution)/shard_map/convert_element_type | solution.py:64
  185.2 7.6 %copy.29 = bf16[4096,576]{1,0:T(8,128)(2,1)} copy(bf16[4096,576]{0,1:T(8,128)(2,1)} %multiply_convert_fusion) | data formatting | bytes 9437184 | tf_op jit(solution)/shard_map/convert_element_type | solution.py:64
  192.9 8.2 %copy.32 = bf16[256,16,576]{0,2,1:T(8,128)(2,1)} copy(bf16[256,16,576]{2,1,0:T(8,128)(2,1)} %bitcast.78) | data formatting | bytes 9437184
  201.1 1.1 convolution_convert_fusion
  202.2 23.3 %reduce-scatter.5.cloned.1.call-done = f32[72,1792]{1,0:T(8,128)} async-done(((f32[576,1792]{1,0:T(8,128)}), f32[72,1792]{1,0:T(8,128)}) %reduce-scatter.5.cloned.1.call-update) | async-done | bytes 516112 | tf_op jit(solution)/shard_map/reduce_scatter | solution.py:69
  225.6 1.8 convert_element_type.40
  (63 shorter events, 2.1 us)
Async XLA Ops:
  7.2 193.9 %copy-start = (bf16[576,1792]{1,0:T(8,128)(2,1)S(1)}, bf16[576,1792]{1,0:T(8,128)(2,1)}, u32[]{:S(2)}) copy-start(bf16[576,1792]{1,0:T(8,128)(2,1)} %param.17) | copy-start | bytes 6193156
  7.2 157.1 %reduce-scatter.7.cloned.1.call-start = ((), (), s32[]{:S(2)}) async-start(), calls=%async_computation.3 | async-start | bytes 1474560 | tf_op jit(solution)/shard_map/reduce_scatter | solution.py:67
  8.2 4.8 %copy-start.5 = (f32[256,16]{1,0:T(8,128)}, f32[256,16]{1,0:T(8,128)S(1)}, u32[]{:S(2)}) copy-start(f32[256,16]{1,0:T(8,128)S(1)} %copy.28) | copy-start | bytes 49156
  8.3 4.8 %copy-start.8 = (bf16[16,576]{1,0:T(8,128)(2,1)S(1)}, bf16[16,576]{1,0:T(8,128)(2,1)}, u32[]{:S(2)}) copy-start(bf16[16,576]{1,0:T(8,128)(2,1)} %param.15) | copy-start | bytes 55300
  86.3 9.0 %copy-start.7 = (s32[256]{0:T(256)S(1)}, s32[256]{0:T(256)}, u32[]{:S(2)}) copy-start(s32[256]{0:T(256)} %param.14) | copy-start | bytes 3076
  96.7 4.6 %copy-start.2 = (bf16[4096,512]{1,0:T(8,128)(2,1)S(1)}, bf16[4096,512]{1,0:T(8,128)(2,1)}, u32[]{:S(2)}) copy-start(bf16[4096,512]{1,0:T(8,128)(2,1)} %get-tuple-element.366) | copy-start | bytes 12582916 | tf_op jit(solution)/shard_map/while
  96.7 7.8 %slice-start.3 = ((s8[5242880]{0:T(1024)(128)(4,1)}), s8[4194304]{0:T(1024)(128)(4,1)S(1)}, s32[]{:S(2)}) async-start(s8[5242880]{0:T(1024)(128)(4,1)} %bitcast.81), calls=%async_computation.7 | async-start | bytes 8388608 | tf_op jit(solution)/shard_map/while
  101.4 3.2 %slice-start.4 = ((s8[5242880]{0:T(1024)(128)(4,1)}), s8[1048576]{0:T(1024)(128)(4,1)S(1)}, s32[]{:S(2)}) async-start(s8[5242880]{0:T(1024)(128)(4,1)} %bitcast.81), calls=%async_computation.8 | async-start | bytes 2097152 | tf_op jit(solution)/shard_map/while
  103.2 1.4 copy-start.3
  103.2 3.5 %slice-start = ((s8[9437184]{0:T(1024)(128)(4,1)}), s8[4194304]{0:T(1024)(128)(4,1)S(1)}, s32[]{:S(2)}) async-start(s8[9437184]{0:T(1024)(128)(4,1)} %bitcast.75), calls=%async_computation.4 | async-start | bytes 8388608 | tf_op jit(solution)/shard_map/while
  103.2 3.8 %slice-start.1 = ((s8[9437184]{0:T(1024)(128)(4,1)}), s8[4194304]{0:T(1024)(128)(4,1)S(1)}, s32[]{:S(2)}) async-start(s8[9437184]{0:T(1024)(128)(4,1)} %bitcast.75), calls=%async_computation.5 | async-start | bytes 8388608 | tf_op jit(solution)/shard_map/while
  104.6 2.9 %slice-start.2 = ((s8[9437184]{0:T(1024)(128)(4,1)}), s8[1048576]{0:T(1024)(128)(4,1)S(1)}, s32[]{:S(2)}) async-start(s8[9437184]{0:T(1024)(128)(4,1)} %bitcast.75), calls=%async_computation.6 | async-start | bytes 2097152 | tf_op jit(solution)/shard_map/while
  107.5 2.6 %copy-start.4 = (f32[2,256,576]{1,2,0:T(8,128)}, f32[2,256,576]{1,2,0:T(8,128)S(1)}, u32[]{:S(2)}) copy-start(f32[2,256,576]{1,2,0:T(8,128)S(1)} %fusion.72) | copy-start | bytes 3538948 | tf_op jit(solution)/shard_map/while
  110.0 3.7 %copy-start.1 = (f32[4096,576]{0,1:T(8,128)}, f32[4096,576]{0,1:T(8,128)S(1)}, u32[]{:S(2)}) copy-start(f32[4096,576]{0,1:T(8,128)S(1)} %select_add_fusion.3) | copy-start | bytes 28311556 | tf_op jit(solution)/shard_map/while
  115.2 4.6 %copy-start.2 = (bf16[4096,512]{1,0:T(8,128)(2,1)S(1)}, bf16[4096,512]{1,0:T(8,128)(2,1)}, u32[]{:S(2)}) copy-start(bf16[4096,512]{1,0:T(8,128)(2,1)} %get-tuple-element.366) | copy-start | bytes 12582916 | tf_op jit(solution)/shard_map/while
  115.2 7.8 %slice-start.3 = ((s8[5242880]{0:T(1024)(128)(4,1)}), s8[4194304]{0:T(1024)(128)(4,1)S(1)}, s32[]{:S(2)}) async-start(s8[5242880]{0:T(1024)(128)(4,1)} %bitcast.81), calls=%async_computation.7 | async-start | bytes 8388608 | tf_op jit(solution)/shard_map/while
  119.8 3.2 %slice-start.4 = ((s8[5242880]{0:T(1024)(128)(4,1)}), s8[1048576]{0:T(1024)(128)(4,1)S(1)}, s32[]{:S(2)}) async-start(s8[5242880]{0:T(1024)(128)(4,1)} %bitcast.81), calls=%async_computation.8 | async-start | bytes 2097152 | tf_op jit(solution)/shard_map/while
  121.7 1.4 copy-start.3
  121.7 3.5 %slice-start = ((s8[9437184]{0:T(1024)(128)(4,1)}), s8[4194304]{0:T(1024)(128)(4,1)S(1)}, s32[]{:S(2)}) async-start(s8[9437184]{0:T(1024)(128)(4,1)} %bitcast.75), calls=%async_computation.4 | async-start | bytes 8388608 | tf_op jit(solution)/shard_map/while
  121.7 3.8 %slice-start.1 = ((s8[9437184]{0:T(1024)(128)(4,1)}), s8[4194304]{0:T(1024)(128)(4,1)S(1)}, s32[]{:S(2)}) async-start(s8[9437184]{0:T(1024)(128)(4,1)} %bitcast.75), calls=%async_computation.5 | async-start | bytes 8388608 | tf_op jit(solution)/shard_map/while
  123.0 2.9 %slice-start.2 = ((s8[9437184]{0:T(1024)(128)(4,1)}), s8[1048576]{0:T(1024)(128)(4,1)S(1)}, s32[]{:S(2)}) async-start(s8[9437184]{0:T(1024)(128)(4,1)} %bitcast.75), calls=%async_computation.6 | async-start | bytes 2097152 | tf_op jit(solution)/shard_map/while
  125.9 2.6 %copy-start.4 = (f32[2,256,576]{1,2,0:T(8,128)}, f32[2,256,576]{1,2,0:T(8,128)S(1)}, u32[]{:S(2)}) copy-start(f32[2,256,576]{1,2,0:T(8,128)S(1)} %fusion.72) | copy-start | bytes 3538948 | tf_op jit(solution)/shard_map/while
  128.5 3.7 %copy-start.1 = (f32[4096,576]{0,1:T(8,128)}, f32[4096,576]{0,1:T(8,128)S(1)}, u32[]{:S(2)}) copy-start(f32[4096,576]{0,1:T(8,128)S(1)} %select_add_fusion.3) | copy-start | bytes 28311556 | tf_op jit(solution)/shard_map/while
  132.2 43.2 %copy-start.6 = (bf16[64,1792]{1,0:T(8,128)(2,1)S(1)}, bf16[64,1792]{1,0:T(8,128)(2,1)}, u32[]{:S(2)}) copy-start(bf16[64,1792]{1,0:T(8,128)(2,1)} %param.16) | copy-start | bytes 688132
  135.0 90.6 %reduce-scatter.5.cloned.1.call-start = ((), (), s32[]{:S(2)}) async-start(), calls=%async_computation.2 | async-start | bytes 4644864 | tf_op jit(solution)/shard_map/reduce_scatter | solution.py:69
Sparse Core Ops, SparseCore 0:
  135.1 29.1 reduce-scatter.6
  178.3 47.2 reduce-scatter.4
